TPU v7x, 32 devices: a whole 2x2x4 slice. The times are simulated.
32 devices in a mesh: rep: 2 (over x), tp: 4 (over y, core), sub: 4 (over z).
Axes of the slice: x: 2, y: 2, z: 4, core: 2. Of those that a mesh axis runs over, the one named last changes fastest.
Arguments:
- acts: bfloat16 [2048, 16384], P(('rep', 'tp'), 'sub'), parts along dimension 0, may hold values from -6 to 6
- q_src: bfloat16 [32768, 16384], P(('rep', 'sub'), 'tp'), parts along dimension 0, may hold values from -0.046875 to 0.046875
- kv_src: bfloat16 [32768, 2048], P(('rep', 'sub'), 'tp'), parts along dimension 0, may hold values from -0.046875 to 0.046875
- q_src_heads: int32 [128], replicated, may hold values from 0 to 127, as said below
- q_tgt_heads: int32 [128], replicated, may hold values from 0 to 127, as said below
- kv_tgt_heads: int32 [16], replicated, may hold values from 0 to 7, as said below
Outputs:
- q_new: bfloat16 [32768, 16384], P(('rep', 'sub'), 'tp'), parts along dimension 0
- kv_new: bfloat16 [32768, 4096], P(('rep', 'sub'), 'tp'), parts along dimension 0
- qkv: bfloat16 [2048, 20480], P(('rep', 'sub'), 'tp'), parts along dimension 0
There are 2 independent parts, one for each index of `rep`. A program takes and returns all parts, laid end to end along the dimension named above; an argument that names none is the same for every part. Nothing has to cross between parts.
Inputs may be any that keep to these rules, and one draw needn't show every extreme that they name: q_src_heads and q_tgt_heads are permutations. Source block t is entries t * 32 to (t + 1) * 32 - 1 of q_src_heads, target block j the same entries of q_tgt_heads. With s = 1, source block t shares exactly 8 heads with target block (t + min(1, s - 1)) mod 4 and with each target block (t + k * s) mod 4 for k from 1 to 3, and none with any other. `q_tgt_heads`: see q_src_heads. `kv_tgt_heads`: every key-value head appears exactly twice.
All inputs are finite; a program needn't handle non-finite values.
Results may differ from a plain program's by a relative error of at most 0.001.
Values may be sent and summed in bfloat16 or wider, within the bound.
A program may use at most 256 MiB of HBM per device.

v0:
```python
import jax
import jax.numpy as jnp
from jax import lax
from jax.sharding import PartitionSpec as P

HD = 128


def per_device(acts, q_src, kv_src, q_src_heads, q_tgt_heads, kv_tgt_heads):
    tp_count = lax.axis_size("tp")
    my_index = lax.axis_index("tp")
    row_count = q_src.shape[0]
    q_local = q_src.shape[1] // HD
    capacity = max(2, q_local // tp_count)
    head_count = q_src_heads.shape[0]
    head_ids = jnp.arange(head_count, dtype=jnp.int32)
    matches = (q_src_heads[None, :] == q_tgt_heads[:, None]).astype(jnp.int32)
    target_pos = jnp.sum(matches * head_ids[:, None], axis=0)
    slot_of = jnp.sum(matches * head_ids[None, :], axis=1)
    target_dev = target_pos // q_local
    source_dev = head_ids // q_local
    earlier = (
        (source_dev[:, None] == source_dev[None, :])
        & (target_dev[:, None] == target_dev[None, :])
        & (head_ids[None, :] < head_ids[:, None])
    )
    slot_rank = jnp.sum(earlier.astype(jnp.int32), axis=1)
    own_target = lax.dynamic_slice_in_dim(target_dev, my_index * q_local, q_local)
    own_rank = lax.dynamic_slice_in_dim(slot_rank, my_index * q_local, q_local)
    buffer_ids = jnp.arange(tp_count * capacity, dtype=jnp.int32)
    slot_hit = ((own_target * capacity + own_rank)[None, :] == buffer_ids[:, None]).astype(
        jnp.int32
    )
    pick_slot = jnp.sum(slot_hit * jnp.arange(q_local, dtype=jnp.int32)[None, :], axis=1)
    filled = jnp.sum(slot_hit, axis=1) > 0
    my_slots = lax.dynamic_slice_in_dim(slot_of, my_index * q_local, q_local)
    receive_ids = my_slots // q_local * capacity + slot_rank[my_slots]

    def pack_heads(weights):
        leading = weights.shape[0]
        three = weights.reshape(leading, q_local, HD)
        packed = jnp.take(three, pick_slot, axis=1) * filled[None, :, None].astype(weights.dtype)
        return packed.reshape(leading, tp_count, capacity * HD)

    def unpack_heads(arrived):
        leading = arrived.shape[0]
        three = arrived.reshape(leading, tp_count * capacity, HD)
        return jnp.take(three, receive_ids, axis=1).reshape(leading, q_local * HD)

    q_arrived = lax.all_to_all(pack_heads(q_src), "tp", split_axis=1, concat_axis=1, tiled=True)
    q_new = unpack_heads(q_arrived)
    kv_slots = kv_tgt_heads.shape[0] // tp_count
    kv_whole = lax.all_gather(kv_src, "tp", axis=1, tiled=True)
    own_kv = lax.dynamic_slice_in_dim(kv_tgt_heads, my_index * kv_slots, kv_slots)
    kv_three = kv_whole.reshape(row_count, kv_whole.shape[1] // (2 * HD), 2 * HD)
    kv_new = jnp.take(kv_three, own_kv, axis=1).reshape(row_count, kv_slots * 2 * HD)
    gathered = lax.all_gather(acts, "tp", axis=0, tiled=True)

    def projector(weights):
        return jnp.dot(gathered, weights, preferred_element_type=jnp.float32)

    q_out = lax.psum_scatter(projector(q_src), "sub", scatter_dimension=0, tiled=True).astype(
        jnp.bfloat16
    )
    q_moved = lax.all_to_all(pack_heads(q_out), "tp", split_axis=1, concat_axis=1, tiled=True)
    kv_out = lax.psum_scatter(projector(kv_new), "sub", scatter_dimension=0, tiled=True).astype(
        jnp.bfloat16
    )
    qkv = jnp.concatenate([unpack_heads(q_moved), kv_out], axis=1)
    return (q_new, kv_new, qkv)


def solution(mesh):
    in_specs = (
        P(("rep", "tp"), "sub"),
        P(("rep", "sub"), "tp"),
        P(("rep", "sub"), "tp"),
        P(),
        P(),
        P(),
    )
    out_specs = (P(("rep", "sub"), "tp"), P(("rep", "sub"), "tp"), P(("rep", "sub"), "tp"))
    return jax.shard_map(
        per_device, mesh=mesh, in_specs=in_specs, out_specs=out_specs, check_vma=False
    )
```

profile of v0, /device:TPU:0, one launch (start us, length us, event | category | flops | bytes accessed | tf_op | source)
XLA Modules:
  0.0 703.1 jit_solution(10137896972993409188)
XLA Ops:
  8.7 61.9 %all-gather.5.cloned.1.call-done = bf16[1024,4096]{1,0:T(8,128)(2,1)} async-done(((bf16[256,4096]{1,0:T(8,128)(2,1)}), bf16[1024,4096]{1,0:T(8,128)(2,1)}) %all-gather.5.cloned.1.call-update) | async-done | bytes 8388624 | tf_op jit(solution)/shard_map/all_gather | solution.py:57
  70.6 43.0 %fusion.4 = f32[1024,4096]{1,0:T(8,128)} fusion(bf16[1024,4096]{1,0:T(8,128)(2,1)} %all-gather.5.cloned.1.call-done, bf16[4096,4096]{1,0:T(8,128)(2,1)} %param.11), kind=kOutput, calls=%fused_computation.53 | convolution fusion | flops 34359738368 | bytes 58720256 | tf_op jit(solution)/shard_map/dot_general | solution.py:60
  113.6 44.2 %copy.27 = bf16[4096,4096]{0,1:T(8,128)(2,1)} copy(bf16[4096,4096]{1,0:T(8,128)(2,1)} %param.11) | data formatting | bytes 67108864 | tf_op args[1]
  158.4 22.9 %gather_fusion.3 = bf16[32,4096,128]{1,2,0:T(8,128)(2,1)} fusion(bf16[4096,32,128]{0,2,1:T(8,128)(2,1)} %bitcast.31, s32[1024]{0:T(1024)S(1)} %pad_clamp_fusion.2), kind=kCustom, calls=%fused_computation.clone | custom fusion | bytes 67108992 | tf_op jit(solution)/shard_map/jit(_take)/gather | solution.py:42
  181.3 22.3 %bitcast_multiply_fusion = bf16[4096,32,128]{0,2,1:T(8,128)(2,1)} fusion(bf16[32,4096,128]{1,2,0:T(8,128)(2,1)} %gather_fusion.3, pred[32]{0:T(512)(128)(4,1)S(1)} %compare_and_fusion.1, bf16[32]{0:T(256)(128)(2,1)S(1)} %compare_convert_fusion), kind=kLoop, calls=%fused_computation.7 | loop fusion | flops 33554432 | bytes 67108960 | tf_op jit(solution)/shard_map/mul | solution.py:42
  203.5 9.9 %all-to-all-start = ((bf16[4096,4,1024]{0,2,1:T(8,128)(2,1)}), bf16[4096,4,1024]{0,2,1:T(8,128)(2,1)}, u32[]{:S(2)}, u32[]{:S(2)}) async-start(bf16[4096,4,1024]{0,2,1:T(8,128)(2,1)} %bitcast.33), calls=%async_computation | async-start | bytes 67108864 | tf_op jit(solution)/shard_map/all_to_all | solution.py:50
  213.9 12.0 %fusion.3 = (bf16[2048,2048]{1,0:T(8,128)(2,1)}, bf16[2048,2048]{1,0:T(8,128)(2,1)}) fusion(bf16[4096,2048]{1,0:T(8,128)(2,1)} %all-gather.3.cloned.1.call-done), kind=kLoop, calls=%fused_computation.52 | loop fusion | bytes 33554432 | tf_op jit(solution)/shard_map/jit(_take)/gather | solution.py:56
  226.0 12.3 %copy.29 = bf16[2048,2048]{0,1:T(8,128)(2,1)} copy(bf16[2048,2048]{1,0:T(8,128)(2,1)} %get-tuple-element.23) | data formatting | bytes 16777216 | tf_op jit(solution)/shard_map/jit(_take)/gather | solution.py:56
  238.2 12.5 %copy.28 = bf16[2048,2048]{0,1:T(8,128)(2,1)} copy(bf16[2048,2048]{1,0:T(8,128)(2,1)} %get-tuple-element.22) | data formatting | bytes 16777216 | tf_op jit(solution)/shard_map/jit(_take)/gather | solution.py:56
  250.7 6.5 gather_fusion.2
  257.1 6.4 gather_fusion.1
  263.5 8.0 %pad_maximum_fusion = bf16[4096,4,256]{0,2,1:T(8,128)(2,1)} fusion(bf16[2048,4,256]{0,2,1:T(8,128)(2,1)} %bitcast.37, bf16[2048,4,256]{0,2,1:T(8,128)(2,1)} %bitcast.38), kind=kLoop, calls=%fused_computation.9 | loop fusion | flops 16777216 | bytes 16777216
  271.5 12.0 %copy.30 = bf16[4096,1024]{1,0:T(8,128)(2,1)} copy(bf16[4096,1024]{0,1:T(8,128)(2,1)} %bitcast.34) | data formatting | bytes 16777216 | tf_op jit(solution)/shard_map/jit(_take)/gather | solution.py:56
  283.4 7.5 %broadcast_select_fusion.1 = bf16[4096,1024]{1,0:T(8,128)(2,1)} fusion(bf16[4096,1024]{1,0:T(8,128)(2,1)} %copy.30, pred[1024]{0:T(1024)(128)(4,1)S(1)} %broadcast_in_dim.54), kind=kLoop, calls=%fused_computation.10 | loop fusion | flops 4194304 | bytes 16778240 | tf_op jit(solution)/shard_map/jit(_take)/select_n | solution.py:56
  290.9 15.2 %convolution_bitcast_fusion = f32[1024,1024]{0,1:T(8,128)} fusion(bf16[4096,1024]{1,0:T(8,128)(2,1)} %broadcast_select_fusion.1, bf16[1024,4096]{1,0:T(8,128)(2,1)} %all-gather.5.cloned.1.call-done), kind=kOutput, calls=%fused_computation.12 | convolution fusion | flops 8589934592 | bytes 20971520 | tf_op jit(solution)/shard_map/dot_general | solution.py:60
  307.1 269.2 %all-to-all-done = bf16[4096,4,1024]{0,2,1:T(8,128)(2,1)} async-done(((bf16[4096,4,1024]{0,2,1:T(8,128)(2,1)}), bf16[4096,4,1024]{0,2,1:T(8,128)(2,1)}, u32[]{:S(2)}, u32[]{:S(2)}) %all-to-all-start) | async-done | bytes 33554464 | tf_op jit(solution)/shard_map/all_to_all | solution.py:50
  576.3 23.0 %gather_fusion.4 = bf16[32,4096,128]{1,2,0:T(8,128)(2,1)} fusion(bf16[4096,32,128]{0,2,1:T(8,128)(2,1)} %bitcast.3, s32[1024]{0:T(1024)S(1)} %pad_clamp_fusion.1), kind=kCustom, calls=%fused_computation.2.clone | custom fusion | bytes 67108992 | tf_op jit(solution)/shard_map/jit(_take)/gather | solution.py:48
  606.0 2.9 copy.32
  608.9 3.8 all-to-all-start.1
  612.8 22.8 %broadcast_select_fusion = bf16[32,4096,128]{1,2,0:T(8,128)(2,1)} fusion(bf16[32,4096,128]{1,2,0:T(8,128)(2,1)} %gather_fusion.4, pred[32]{0:T(512)(128)(4,1)S(1)} %get-tuple-element.20), kind=kLoop, calls=%fused_computation.8 | loop fusion | flops 16777216 | bytes 67108896 | tf_op jit(solution)/shard_map/jit(_take)/select_n | solution.py:48
  635.6 44.1 %copy.35 = bf16[4096,4096]{1,0:T(8,128)(2,1)} copy(bf16[4096,4096]{0,1:T(8,128)(2,1)} %bitcast.32) | data formatting | bytes 67108864
  681.0 2.9 copy.33
  688.0 4.1 copy.34
  693.8 2.8 copy.36
  (43 shorter events, 17.3 us)
Async XLA Ops:
  7.2 63.4 %all-gather.5.cloned.1.call-start = ((), (), s32[]{:S(2)}) async-start(), calls=%async_computation.5 | async-start | bytes 10485760 | tf_op jit(solution)/shard_map/all_gather | solution.py:57
  7.9 206.0 %all-gather.3.cloned.1.call-start = ((), (), s32[]{:S(2)}) async-start(), calls=%async_computation.4 | async-start | bytes 20971520 | tf_op jit(solution)/shard_map/all_gather | solution.py:53
  8.6 590.7 %reduce-scatter.3.cloned.1.call-start = ((), (), s32[]{:S(2)}) async-start(), calls=%async_computation.6 | async-start | bytes 20971520 | tf_op jit(solution)/shard_map/reduce_scatter | solution.py:62
  113.6 44.2 %copy-start = (s32[128]{0:T(128)S(1)}, s32[128]{0:T(128)}, u32[]{:S(2)}) copy-start(s32[128]{0:T(128)} %param.13) | copy-start | bytes 1540
  113.6 44.2 %copy-start.1 = (s32[128]{0:T(128)S(1)}, s32[128]{0:T(128)}, u32[]{:S(2)}) copy-start(s32[128]{0:T(128)} %param.14) | copy-start | bytes 1540
  203.5 10.2 %copy-start.2 = (s32[16]{0:T(128)S(1)}, s32[16]{0:T(128)}, u32[]{:S(2)}) copy-start(s32[16]{0:T(128)} %param.15) | copy-start | bytes 196
  203.5 372.7 %all-to-all-start = ((bf16[4096,4,1024]{0,2,1:T(8,128)(2,1)}), bf16[4096,4,1024]{0,2,1:T(8,128)(2,1)}, u32[]{:S(2)}, u32[]{:S(2)}) async-start(bf16[4096,4,1024]{0,2,1:T(8,128)(2,1)} %bitcast.33), calls=%async_computation | async-start | bytes 67108864 | tf_op jit(solution)/shard_map/all_to_all | solution.py:50
  213.5 466.2 %reduce-scatter.5.cloned.1.call-start = ((), (), s32[]{:S(2)}) async-start(), calls=%async_computation.7 | async-start | bytes 5242880 | tf_op jit(solution)/shard_map/reduce_scatter | solution.py:66
  608.9 72.0 %all-to-all-start.1 = ((bf16[256,4,1024]{0,2,1:T(8,128)(2,1)}), bf16[256,4,1024]{0,2,1:T(8,128)(2,1)S(1)}, u32[]{:S(2)}, u32[]{:S(2)}) async-start(bf16[256,4,1024]{0,2,1:T(8,128)(2,1)} %bitcast.40), calls=%async_computation.2 | async-start | bytes 4194304 | tf_op jit(solution)/shard_map/all_to_all | solution.py:65
Sparse Core Ops, SparseCore 0:
  9.5 60.9 all-gather.4
  72.1 105.8 all-gather.2
  180.4 280.4 reduce-scatter.2
  463.0 77.3 reduce-scatter.4
where the time goes:
time: 707 us; the launch traced here: 703 us
  waiting for transfers between devices  332 us (47%)
  local copies, waits for them, and re-layouts  214 us (30%)
  other arithmetic  70.6 us (10%)
  matrix products  58.2 us (8%)
  starting transfers between devices  14.1 us (2%)
  between operations  13.9 us (2%)
    all_to_all x1, waiting for transfers between devices, per_device(): lax.all_to_all(pack_heads(q_src), 'tp', split_axis=1, concat_axis=1, tile...  269 us
    unnamed x9, local copies, waits for them, and re-layouts  91 us
    all_gather x1, waiting for transfers between devices, per_device(): gathered = lax.all_gather(acts, 'tp', axis=0, tiled=True)  61.9 us
    gather x6, local copies, waits for them, and re-layouts, per_device(): jnp.take(kv_three, own_kv, axis=1).reshape(row_count, kv_slots * 2 * HD)  61.5 us
    dot_general x2, matrix products, projector(): return jnp.dot(gathered, weights, preferred_element_type=jnp.float32)  58.2 us
    gather x2, local copies, waits for them, and re-layouts, unpack_heads(): return jnp.take(three, receive_ids, axis=1).reshape(leading, q_local * HD)  25.6 us
    gather x2, local copies, waits for them, and re-layouts, pack_heads(): jnp.take(three, pick_slot, axis=1)  25 us
    select_n x2, other arithmetic, unpack_heads(): return jnp.take(three, receive_ids, axis=1).reshape(leading, q_local * HD)  24.4 us
  transfers between devices with their start and end apart: 6, of which 2 were waited for; matrix products, arithmetic and copies ran while one was open for 47% of the time, Pallas kernels for 0%

commit v1 on v0

v1 whole, which is shorter than its diff:
```python
import functools

import jax
import jax.numpy as jnp
from jax import lax
from jax.experimental import pallas as pl
from jax.experimental.pallas import tpu as pltpu
from jax.sharding import PartitionSpec as P


HD = 128
ROW_CHUNKS = 4
BLOCK_ROWS = 256


def cost(nbytes):
    return pl.CostEstimate(flops=0, bytes_accessed=nbytes, transcendentals=0)


def pack_body(n, cap, pick, x_ref, *outs):
    for o in range(n):
        for r in range(cap):
            start = pl.multiple_of(pick[o * cap + r] * HD, HD)
            outs[o][:, r * HD : (r + 1) * HD] = x_ref[:, pl.ds(start, HD)].astype(outs[o].dtype)


def pack(x, pick, n, cap, first_row, rows):
    width = x.shape[1]
    block = min(BLOCK_ROWS, rows)
    skip = first_row // block
    return pl.pallas_call(
        functools.partial(pack_body, n, cap),
        grid_spec=pltpu.PrefetchScalarGridSpec(
            num_scalar_prefetch=1,
            grid=(rows // block,),
            in_specs=[pl.BlockSpec((block, width), lambda i, p: (skip + i, 0))],
            out_specs=[pl.BlockSpec((block, cap * HD), lambda i, p: (i, 0))] * n,
        ),
        out_shape=[jax.ShapeDtypeStruct((rows, cap * HD), jnp.bfloat16)] * n,
        cost_estimate=cost(rows * (width + n * cap * HD) * 2),
    )(pick, x)


def unpack_body(n, cap, full, has_extra, dest, *refs):
    out = refs[-1]
    for o in range(n):
        for r in range(cap):
            place = dest[o * cap + r]

            def put(o=o, r=r, place=place):
                out[:, pl.ds(pl.multiple_of(place * HD, HD), HD)] = refs[o][:, r * HD : (r + 1) * HD]

            if full:
                put()
            else:
                pl.when(place >= 0)(put)
    if has_extra:
        extra = refs[n]
        out[:, out.shape[1] - extra.shape[1] :] = extra[...].astype(out.dtype)


def unpack(pieces, dest, q_local, cap, first_row, total_rows, before=None, extra=None):
    n, rows = len(pieces), pieces[0].shape[0]
    block = min(BLOCK_ROWS, rows)
    skip = first_row // block
    width = q_local * HD + (extra.shape[1] if extra is not None else 0)
    in_specs = [pl.BlockSpec((block, cap * HD), lambda i, d: (i, 0))] * n
    operands = list(pieces)
    aliases = {}
    if extra is not None:
        in_specs.append(pl.BlockSpec((block, extra.shape[1]), lambda i, d: (i, 0)))
        operands.append(extra)
    if before is not None:
        aliases = {1 + len(operands): 0}
        in_specs.append(pl.BlockSpec(memory_space=pl.ANY))
        operands.append(before)
    return pl.pallas_call(
        functools.partial(unpack_body, n, cap, n * cap == q_local, extra is not None),
        grid_spec=pltpu.PrefetchScalarGridSpec(
            num_scalar_prefetch=1,
            grid=(rows // block,),
            in_specs=in_specs,
            out_specs=pl.BlockSpec((block, width), lambda i, d: (skip + i, 0)),
        ),
        out_shape=jax.ShapeDtypeStruct((total_rows, width), jnp.bfloat16),
        input_output_aliases=aliases,
        cost_estimate=cost(rows * width * 4),
    )(dest, *operands)


def choose_body(n, units, piece_of, unit_of, *refs):
    out = refs[-1]
    for k in range(units):
        for o in range(n):

            @pl.when(piece_of[k] == o)
            def _(k=k, o=o):
                start = pl.multiple_of(unit_of[k] * HD, HD)
                out[:, k * HD : (k + 1) * HD] = refs[o][:, pl.ds(start, HD)]


def choose(pieces, piece_of, unit_of):
    n, (rows, width) = len(pieces), pieces[0].shape
    units = piece_of.shape[0]
    block = min(BLOCK_ROWS, rows)
    return pl.pallas_call(
        functools.partial(choose_body, n, units),
        grid_spec=pltpu.PrefetchScalarGridSpec(
            num_scalar_prefetch=2,
            grid=(rows // block,),
            in_specs=[pl.BlockSpec((block, width), lambda i, a, b: (i, 0))] * n,
            out_specs=pl.BlockSpec((block, units * HD), lambda i, a, b: (i, 0)),
        ),
        out_shape=jax.ShapeDtypeStruct((rows, units * HD), jnp.bfloat16),
        cost_estimate=cost(rows * (n * width + units * HD) * 2),
    )(piece_of, unit_of, *pieces)


def layer(acts, q_src, kv_src, q_src_heads, q_tgt_heads, kv_tgt_heads):
    n = lax.axis_size("tp")
    me = lax.axis_index("tp").astype(jnp.int32)
    rows = q_src.shape[0]
    q_local = q_src.shape[1] // HD
    cap = max(2, q_local // n)

    def swap(x, o):
        return lax.ppermute(x, "tp", [(i, i ^ o) for i in range(n)])

    def exchange(x):
        pieces = {0: x}
        pieces[1] = swap(x, 1)
        for o in range(2, n, 2):
            pieces[o] = swap(x, o)
        for o in range(2, n, 2):
            pieces[o + 1] = swap(pieces[o], 1)
        return [pieces[o] for o in range(n)]

    act_pieces = exchange(acts)
    kv_pieces = exchange(kv_src)

    ids = jnp.arange(q_src_heads.shape[0], dtype=jnp.int32)
    slot_of = jnp.sum(
        jnp.where(q_tgt_heads[:, None] == q_src_heads[None, :], ids[None, :], 0), axis=1
    )
    source_dev = slot_of // q_local
    target_dev = ids // q_local
    earlier = (
        (source_dev[:, None] == source_dev[None, :])
        & (target_dev[:, None] == target_dev[None, :])
        & (ids[None, :] < ids[:, None])
    )
    rank = jnp.sum(earlier.astype(jnp.int32), axis=1)
    buffer_ids = jnp.arange(n * cap, dtype=jnp.int32)
    send_at = jnp.where(source_dev == me, (target_dev ^ me) * cap + rank, -1)
    pick = jnp.sum(
        jnp.where(send_at[None, :] == buffer_ids[:, None], slot_of[None, :] - me * q_local, 0), axis=1
    )
    receive_at = jnp.where(target_dev == me, (source_dev ^ me) * cap + rank, -1)
    dest = (
        jnp.sum(
            jnp.where(
                receive_at[None, :] == buffer_ids[:, None], ids[None, :] - me * q_local + 1, 0
            ),
            axis=1,
        )
        - 1
    )

    chunks = ROW_CHUNKS if rows % (ROW_CHUNKS * BLOCK_ROWS) == 0 else 1
    chunk_rows = rows // chunks
    packed = [pack(q_src, pick, n, cap, c * chunk_rows, chunk_rows) for c in range(chunks)]
    arrived = [[p[0]] + [swap(p[o], o) for o in range(1, n)] for p in packed]

    tokens = acts.shape[0]
    gathered = jnp.zeros((n * tokens, acts.shape[1]), acts.dtype)
    for o in range(n):
        gathered = lax.dynamic_update_slice_in_dim(gathered, act_pieces[o], (me ^ o) * tokens, 0)

    def project(weights):
        full = jnp.dot(gathered, weights, preferred_element_type=jnp.float32)
        return lax.psum_scatter(full, "sub", scatter_dimension=0, tiled=True)

    q_out = project(q_src)

    kv_slots = kv_tgt_heads.shape[0] // n
    per_dev = kv_src.shape[1] // HD
    own_kv = lax.dynamic_slice_in_dim(kv_tgt_heads, me * kv_slots, kv_slots)
    units = (2 * own_kv[:, None] + jnp.arange(2, dtype=jnp.int32)[None, :]).reshape(-1)
    kv_new = choose(kv_pieces, (units // per_dev) ^ me, units % per_dev)
    kv_out = project(kv_new)

    q_new = None
    for c in range(chunks):
        q_new = unpack(arrived[c], dest, q_local, cap, c * chunk_rows, rows, before=q_new)

    out_rows = q_out.shape[0]
    q_packed = pack(q_out, pick, n, cap, 0, out_rows)
    q_moved = [q_packed[0]] + [swap(q_packed[o], o) for o in range(1, n)]
    qkv = unpack(q_moved, dest, q_local, cap, 0, out_rows, extra=kv_out)
    return (q_new, kv_new, qkv)


def solution(mesh):
    in_specs = (
        P(("rep", "tp"), "sub"),
        P(("rep", "sub"), "tp"),
        P(("rep", "sub"), "tp"),
        P(),
        P(),
        P(),
    )
    out_specs = (P(("rep", "sub"), "tp"), P(("rep", "sub"), "tp"), P(("rep", "sub"), "tp"))
    return jax.shard_map(layer, mesh=mesh, in_specs=in_specs, out_specs=out_specs, check_vma=False)
```

time: 707 us -> 646 us (0.914)
  local copies, waits for them, and re-layouts: 214 us -> 9.83 us
  waiting for transfers between devices: 332 us -> 452 us
  Pallas kernels: 0 us -> 94.1 us
  other arithmetic: 70.6 us -> 2.44 us
    ppermute x0 -> x21, waiting for transfers between devices: none -> 452 us  [swap(): return lax.ppermute(x, 'tp', [(i, i ^ o) for i in range(n)])]
    all_to_all x2 -> x0, waiting for transfers between devices: 269 us -> none  [the longest x1 269 us: per_device(): lax.all_to_all(pack_heads(q_src), 'tp', split_axis=1, concat_axis=1, tile...]
    gather x11 -> x0, local copies, waits for them, and re-layouts: 113 us -> none  [the longest x6 61.5 us: per_device(): jnp.take(kv_three, own_kv, axis=1).reshape(row_count, kv_slots * 2 * HD)]
    pallas_call x0 -> x11, Pallas kernels: none -> 94.1 us  [the longest x5 39.7 us: pack(): pl.pallas_call(functools.partial(pack_body, n, cap), grid_spec=pltpu.Pref...]
    unnamed x9 -> x18, local copies, waits for them, and re-layouts: 91 us -> 4.47 us
    all_gather x2 -> x0, waiting for transfers between devices: 61.9 us -> none  [the longest x1 61.9 us: per_device(): gathered = lax.all_gather(acts, 'tp', axis=0, tiled=True)]
    select_n x6 -> x3, other arithmetic: 32 us -> 0.61 us  [the longest x1 0.6 us: layer(): kv_new = choose(kv_pieces, units // per_dev ^ me, units % per_dev)]
    mul x2 -> x1, other arithmetic: 24.2 us -> 0.07 us  [layer(): 2 * own_kv[:, None] + jnp.arange(2, dtype=jnp.int32)[None, :]]
  transfers between devices with their start and end apart: 6 -> 23, of which waited for: 2 -> 14; matrix products, arithmetic and copies ran while one was open for 47% -> 3% of each run, Pallas kernels for 0% -> 14%
where the time goes in v1:
time: 646 us; the launch traced here: 645 us
  waiting for transfers between devices  452 us (70%)
  Pallas kernels  94.1 us (15%)
  matrix products  55.9 us (9%)
  starting transfers between devices  16 us (2%)
  between operations  14.2 us (2%)
  local copies, waits for them, and re-layouts  9.83 us (2%)
    ppermute x21, waiting for transfers between devices, swap(): return lax.ppermute(x, 'tp', [(i, i ^ o) for i in range(n)])  452 us
    dot_general x2, matrix products, project(): full = jnp.dot(gathered, weights, preferred_element_type=jnp.float32)  55.9 us
    pallas_call x5, Pallas kernels, pack(): pl.pallas_call(functools.partial(pack_body, n, cap), grid_spec=pltpu.Pref...  39.7 us
    pallas_call x5, Pallas kernels, unpack(): pl.pallas_call(functools.partial(unpack_body, n, cap, n * cap == q_local,...  38 us
    pallas_call x1, Pallas kernels, choose(): pl.pallas_call(functools.partial(choose_body, n, units), grid_spec=pltpu....  16.4 us
    ppermute x21, starting transfers between devices, swap(): return lax.ppermute(x, 'tp', [(i, i ^ o) for i in range(n)])  15.8 us
  transfers between devices with their start and end apart: 23, of which 14 were waited for; matrix products, arithmetic and copies ran while one was open for 3% of the time, Pallas kernels for 14%

profile of v1, /device:TPU:0, one launch (start us, length us, event | category | flops | bytes accessed | tf_op | source)
XLA Modules:
  0.0 644.9 jit_solution(13901381681934183164)
XLA Ops:
  10.3 45.8 %collective-permute-done.16 = bf16[256,4096]{1,0:T(8,128)(2,1)S(1)} collective-permute-done((bf16[256,4096]{1,0:T(8,128)(2,1)}, bf16[256,4096]{1,0:T(8,128)(2,1)S(1)}, u32[]{:S(2)}, u32[]{:S(2)}) %collective-permute-start.16) | collective-permute-done | bytes 2097184 | tf_op jit(solution)/shard_map/ppermute | solution.py:127
  65.5 40.9 %fusion.2 = f32[1024,4096]{1,0:T(8,128)} fusion(bf16[1024,4096]{1,0:T(8,128)(2,1)S(1)} %constant_dynamic-update-slice_fusion.3, bf16[4096,4096]{1,0:T(8,128)(2,1)} %x_ref.7), kind=kOutput, calls=%fused_computation.33 | convolution fusion | flops 34359738368 | bytes 58720256 | tf_op jit(solution)/shard_map/dot_general | solution.py:180
  108.5 91.3 %collective-permute-done.13.refs_2_ = bf16[4096,512]{1,0:T(8,128)(2,1)} collective-permute-done((bf16[4096,512]{1,0:T(8,128)(2,1)}, bf16[4096,512]{1,0:T(8,128)(2,1)}, u32[]{:S(2)}, u32[]{:S(2)}) %collective-permute-start.13) | collective-permute-done | bytes 4194336 | tf_op jit(solution)/shard_map/ppermute | solution.py:127
  200.6 6.7 %collective-permute-done.14.refs_3_ = bf16[4096,512]{1,0:T(8,128)(2,1)} collective-permute-done((bf16[4096,512]{1,0:T(8,128)(2,1)}, bf16[4096,512]{1,0:T(8,128)(2,1)}, u32[]{:S(2)}, u32[]{:S(2)}) %collective-permute-start.14) | collective-permute-done | bytes 4194336 | tf_op jit(solution)/shard_map/ppermute | solution.py:127
  207.3 16.4 %shard_map.93 = bf16[4096,1024]{1,0:T(8,128)(2,1)} custom-call(s32[8]{0:T(128)} %get-tuple-element.46.piece_of, s32[8]{0:T(128)} %get-tuple-element.45.unit_of, bf16[4096,512]{1,0:T(8,128)(2,1)} %refs_0_.1, bf16[4096,512]{1,0:T(8,128)(2,1)} %collective-permute-done.12.refs_1_, bf16[4096,512]{1,0:T(8,128)(2,1)} %collective-permute-done.13.refs_2_, ...), custom_call_target="tpu_custom_call" | custom-call | bytes 25165824 | tf_op jit(solution)/shard_map/pallas_call | solution.py:106
  223.6 15.0 %fusion.3 = f32[1024,1024]{1,0:T(8,128)} fusion(bf16[1024,4096]{1,0:T(8,128)(2,1)} %copy-done, bf16[4096,1024]{1,0:T(8,128)(2,1)} %shard_map.93), kind=kOutput, calls=%fused_computation.34 | convolution fusion | flops 8589934592 | bytes 20971520 | tf_op jit(solution)/shard_map/dot_general | solution.py:180
  240.4 8.7 %shard_map.88 = (bf16[1024,1024]{1,0:T(8,128)(2,1)}, bf16[1024,1024]{1,0:T(8,128)(2,1)}, bf16[1024,1024]{1,0:T(8,128)(2,1)}, bf16[1024,1024]{1,0:T(8,128)(2,1)}) custom-call(s32[32]{0:T(128)} %select_reduce_fusion.1.pick, bf16[4096,4096]{1,0:T(8,128)(2,1)} %x_ref.7), custom_call_target="tpu_custom_call" | custom-call | bytes 16777216 | tf_op jit(solution)/shard_map/pallas_call | solution.py:31
  251.2 9.0 %shard_map.87 = (bf16[1024,1024]{1,0:T(8,128)(2,1)}, bf16[1024,1024]{1,0:T(8,128)(2,1)}, bf16[1024,1024]{1,0:T(8,128)(2,1)}, bf16[1024,1024]{1,0:T(8,128)(2,1)}) custom-call(s32[32]{0:T(128)} %select_reduce_fusion.1.pick, bf16[4096,4096]{1,0:T(8,128)(2,1)} %x_ref.7), custom_call_target="tpu_custom_call" | custom-call | bytes 16777216 | tf_op jit(solution)/shard_map/pallas_call | solution.py:31
  261.8 8.6 %shard_map.86 = (bf16[1024,1024]{1,0:T(8,128)(2,1)}, bf16[1024,1024]{1,0:T(8,128)(2,1)}, bf16[1024,1024]{1,0:T(8,128)(2,1)}, bf16[1024,1024]{1,0:T(8,128)(2,1)}) custom-call(s32[32]{0:T(128)} %select_reduce_fusion.1.pick, bf16[4096,4096]{1,0:T(8,128)(2,1)} %x_ref.7), custom_call_target="tpu_custom_call" | custom-call | bytes 16777216 | tf_op jit(solution)/shard_map/pallas_call | solution.py:31
  270.4 27.3 %collective-permute-done.10.refs_2_ = bf16[1024,1024]{1,0:T(8,128)(2,1)S(1)} collective-permute-done((bf16[1024,1024]{1,0:T(8,128)(2,1)}, bf16[1024,1024]{1,0:T(8,128)(2,1)S(1)}, u32[]{:S(2)}, u32[]{:S(2)}) %collective-permute-start.10) | collective-permute-done | bytes 2097184 | tf_op jit(solution)/shard_map/ppermute | solution.py:127
  298.0 44.0 %collective-permute-done.11.refs_3_ = bf16[1024,1024]{1,0:T(8,128)(2,1)} collective-permute-done((bf16[1024,1024]{1,0:T(8,128)(2,1)}, bf16[1024,1024]{1,0:T(8,128)(2,1)}, u32[]{:S(2)}, u32[]{:S(2)}) %collective-permute-start.11) | collective-permute-done | bytes 2097184 | tf_op jit(solution)/shard_map/ppermute | solution.py:127
  342.9 8.7 %shard_map.85 = (bf16[1024,1024]{1,0:T(8,128)(2,1)}, bf16[1024,1024]{1,0:T(8,128)(2,1)}, bf16[1024,1024]{1,0:T(8,128)(2,1)}, bf16[1024,1024]{1,0:T(8,128)(2,1)}) custom-call(s32[32]{0:T(128)} %select_reduce_fusion.1.pick, bf16[4096,4096]{1,0:T(8,128)(2,1)} %x_ref.7), custom_call_target="tpu_custom_call" | custom-call | bytes 16777216 | tf_op jit(solution)/shard_map/pallas_call | solution.py:31
  353.3 34.5 %collective-permute-done.7.refs_2_ = bf16[1024,1024]{1,0:T(8,128)(2,1)} collective-permute-done((bf16[1024,1024]{1,0:T(8,128)(2,1)}, bf16[1024,1024]{1,0:T(8,128)(2,1)}, u32[]{:S(2)}, u32[]{:S(2)}) %collective-permute-start.7) | collective-permute-done | bytes 2097184 | tf_op jit(solution)/shard_map/ppermute | solution.py:127
  387.8 44.1 %collective-permute-done.8.refs_3_ = bf16[1024,1024]{1,0:T(8,128)(2,1)} collective-permute-done((bf16[1024,1024]{1,0:T(8,128)(2,1)}, bf16[1024,1024]{1,0:T(8,128)(2,1)}, u32[]{:S(2)}, u32[]{:S(2)}) %collective-permute-start.8) | collective-permute-done | bytes 2097184 | tf_op jit(solution)/shard_map/ppermute | solution.py:127
  434.2 4.8 shard_map.94
  438.9 38.6 %collective-permute-done.4.refs_2_ = bf16[1024,1024]{1,0:T(8,128)(2,1)S(1)} collective-permute-done((bf16[1024,1024]{1,0:T(8,128)(2,1)}, bf16[1024,1024]{1,0:T(8,128)(2,1)S(1)}, u32[]{:S(2)}, u32[]{:S(2)}) %collective-permute-start.4) | collective-permute-done | bytes 2097184 | tf_op jit(solution)/shard_map/ppermute | solution.py:127
  477.5 44.2 %collective-permute-done.5.refs_3_ = bf16[1024,1024]{1,0:T(8,128)(2,1)} collective-permute-done((bf16[1024,1024]{1,0:T(8,128)(2,1)}, bf16[1024,1024]{1,0:T(8,128)(2,1)}, u32[]{:S(2)}, u32[]{:S(2)}) %collective-permute-start.5) | collective-permute-done | bytes 2097184 | tf_op jit(solution)/shard_map/ppermute | solution.py:127
  524.4 8.3 %shard_map.89.refs_4_ = bf16[4096,4096]{1,0:T(8,128)(2,1)} custom-call(s32[32]{0:T(128)} %broadcast_add_fusion.dest, bf16[1024,1024]{1,0:T(8,128)(2,1)} %get-tuple-element.35.refs_0_, bf16[1024,1024]{1,0:T(8,128)(2,1)} %collective-permute-done.9.refs_1_, bf16[1024,1024]{1,0:T(8,128)(2,1)} %copy-done.1, bf16[1024,1024]{1,0:T(8,128)(2,1)} %collective-permute-done.11.refs_3_), custom_call_target="tpu_custom_call" | custom-call | bytes 16777216 | tf_op jit(solution)/shard_map/pallas_call | solution.py:77
  532.8 8.4 %shard_map.90.refs_4_ = bf16[4096,4096]{1,0:T(8,128)(2,1)} custom-call(s32[32]{0:T(128)} %broadcast_add_fusion.dest, bf16[1024,1024]{1,0:T(8,128)(2,1)} %get-tuple-element.31.refs_0_, bf16[1024,1024]{1,0:T(8,128)(2,1)} %collective-permute-done.6.refs_1_, bf16[1024,1024]{1,0:T(8,128)(2,1)} %collective-permute-done.7.refs_2_, ...), custom_call_target="tpu_custom_call", output_to_operand_aliasing={{}: (5, {})} | custom-call | bytes 16777216 | tf_op jit(solution)/shard_map/pallas_call | solution.py:77
  541.1 8.3 %shard_map.91.refs_4_ = bf16[4096,4096]{1,0:T(8,128)(2,1)} custom-call(s32[32]{0:T(128)} %broadcast_add_fusion.dest, bf16[1024,1024]{1,0:T(8,128)(2,1)} %get-tuple-element.27.refs_0_, bf16[1024,1024]{1,0:T(8,128)(2,1)} %collective-permute-done.3.refs_1_, bf16[1024,1024]{1,0:T(8,128)(2,1)} %copy-done.2, ...), custom_call_target="tpu_custom_call", output_to_operand_aliasing={{}: (5, {})} | custom-call | bytes 16777216 | tf_op jit(solution)/shard_map/pallas_call | solution.py:77
  549.5 18.1 %collective-permute-done.1.refs_2_ = bf16[1024,1024]{1,0:T(8,128)(2,1)} collective-permute-done((bf16[1024,1024]{1,0:T(8,128)(2,1)}, bf16[1024,1024]{1,0:T(8,128)(2,1)}, u32[]{:S(2)}, u32[]{:S(2)}) %collective-permute-start.1) | collective-permute-done | bytes 2097184 | tf_op jit(solution)/shard_map/ppermute | solution.py:127
  567.5 44.1 %collective-permute-done.2.refs_3_ = bf16[1024,1024]{1,0:T(8,128)(2,1)} collective-permute-done((bf16[1024,1024]{1,0:T(8,128)(2,1)}, bf16[1024,1024]{1,0:T(8,128)(2,1)}, u32[]{:S(2)}, u32[]{:S(2)}) %collective-permute-start.2) | collective-permute-done | bytes 2097184 | tf_op jit(solution)/shard_map/ppermute | solution.py:127
  611.6 8.3 %shard_map.92 = bf16[4096,4096]{1,0:T(8,128)(2,1)} custom-call(s32[32]{0:T(128)} %broadcast_add_fusion.dest, bf16[1024,1024]{1,0:T(8,128)(2,1)} %get-tuple-element.23.refs_0_, bf16[1024,1024]{1,0:T(8,128)(2,1)} %collective-permute-done.refs_1_, bf16[1024,1024]{1,0:T(8,128)(2,1)} %collective-permute-done.1.refs_2_, ...), custom_call_target="tpu_custom_call", output_to_operand_aliasing={{}: (5, {})} | custom-call | bytes 16777216 | tf_op jit(solution)/shard_map/pallas_call | solution.py:77
  623.6 9.9 %collective-permute-done.20.refs_3_ = bf16[256,1024]{1,0:T(8,128)(2,1)} collective-permute-done((bf16[256,1024]{1,0:T(8,128)(2,1)}, bf16[256,1024]{1,0:T(8,128)(2,1)}, u32[]{:S(2)}, u32[]{:S(2)}) %collective-permute-start.20) | collective-permute-done | bytes 524320 | tf_op jit(solution)/shard_map/ppermute | solution.py:127
  (72 shorter events, 36.8 us)
Async XLA Ops:
  7.2 427.0 %reduce-scatter.3.cloned.1.call-start = ((), (), s32[]{:S(2)}) async-start(), calls=%async_computation.2 | async-start | bytes 20971520 | tf_op jit(solution)/shard_map/reduce_scatter | solution.py:181
  7.2 48.9 %collective-permute-start.16 = (bf16[256,4096]{1,0:T(8,128)(2,1)}, bf16[256,4096]{1,0:T(8,128)(2,1)S(1)}, u32[]{:S(2)}, u32[]{:S(2)}) collective-permute-start(bf16[256,4096]{1,0:T(8,128)(2,1)} %param.6), channel_id=1, source_target_pairs={{0,8},{4,12},{8,0},{12,4},{1,9},{5,13},{9,1},{13,5},{2,10},{6,14},... | collective-permute-start | bytes 6291464 | tf_op jit(solution)/shard_map/ppermute | solution.py:127
  10.3 47.7 %collective-permute-start.15 = (bf16[256,4096]{1,0:T(8,128)(2,1)}, bf16[256,4096]{1,0:T(8,128)(2,1)}, u32[]{:S(2)}, u32[]{:S(2)}) collective-permute-start(bf16[256,4096]{1,0:T(8,128)(2,1)} %param.6), channel_id=1, source_target_pairs={{0,4},{4,0},{8,12},{12,8},{1,5},{5,1},{9,13},{13,9},{2,6},{6,2},{1... | collective-permute-start | bytes 6291464 | tf_op jit(solution)/shard_map/ppermute | solution.py:127
  56.1 4.3 collective-permute-start.17
  106.4 93.4 %copy-start.6 = (s32[16]{0:T(128)S(1)}, s32[16]{0:T(128)}, u32[]{:S(2)}) copy-start(s32[16]{0:T(128)} %param.11) | copy-start | bytes 196
  106.4 513.6 %reduce-scatter.5.cloned.1.call-start = ((), (), s32[]{:S(2)}) async-start(), calls=%async_computation.3 | async-start | bytes 5242880 | tf_op jit(solution)/shard_map/reduce_scatter | solution.py:181
  106.7 93.1 %collective-permute-start.13 = (bf16[4096,512]{1,0:T(8,128)(2,1)}, bf16[4096,512]{1,0:T(8,128)(2,1)}, u32[]{:S(2)}, u32[]{:S(2)}) collective-permute-start(bf16[4096,512]{1,0:T(8,128)(2,1)} %refs_0_.1), channel_id=1, source_target_pairs={{0,8},{4,12},{8,0},{12,4},{1,9},{5,13},{9,1},{13,5},{2,10},{6,14},... | collective-permute-start | bytes 12582920 | tf_op jit(solution)/shard_map/ppermute | solution.py:127
  108.5 92.1 %collective-permute-start.12 = (bf16[4096,512]{1,0:T(8,128)(2,1)}, bf16[4096,512]{1,0:T(8,128)(2,1)}, u32[]{:S(2)}, u32[]{:S(2)}) collective-permute-start(bf16[4096,512]{1,0:T(8,128)(2,1)} %refs_0_.1), channel_id=1, source_target_pairs={{0,4},{4,0},{8,12},{12,8},{1,5},{5,1},{9,13},{13,9},{2,6},{6,2},{1... | collective-permute-start | bytes 12582920 | tf_op jit(solution)/shard_map/ppermute | solution.py:127
  199.8 7.5 %collective-permute-start.14 = (bf16[4096,512]{1,0:T(8,128)(2,1)}, bf16[4096,512]{1,0:T(8,128)(2,1)}, u32[]{:S(2)}, u32[]{:S(2)}) collective-permute-start(bf16[4096,512]{1,0:T(8,128)(2,1)} %collective-permute-done.13.refs_2_), channel_id=1, source_target_pairs={{0,4},{4,0},{8,12},{12,8},{1,5},{5,1},{9,13},{13,9},{2,6},{6,2},{1... | collective-permute-start | bytes 12582920 | tf_op jit(solution)/shard_map/ppermute | solution.py:127
  249.1 48.7 %collective-permute-start.10 = (bf16[1024,1024]{1,0:T(8,128)(2,1)}, bf16[1024,1024]{1,0:T(8,128)(2,1)S(1)}, u32[]{:S(2)}, u32[]{:S(2)}) collective-permute-start(bf16[1024,1024]{1,0:T(8,128)(2,1)} %get-tuple-element.37), channel_id=1, source_target_pairs={{0,8},{4,12},{8,0},{12,4},{1,9},{5,13},{9,1},{13,5},{2,10},{6,14},... | collective-permute-start | bytes 6291464 | tf_op jit(solution)/shard_map/ppermute | solution.py:127
  250.7 91.3 %collective-permute-start.11 = (bf16[1024,1024]{1,0:T(8,128)(2,1)}, bf16[1024,1024]{1,0:T(8,128)(2,1)}, u32[]{:S(2)}, u32[]{:S(2)}) collective-permute-start(bf16[1024,1024]{1,0:T(8,128)(2,1)} %get-tuple-element.38), channel_id=1, source_target_pairs={{0,12},{4,8},{8,4},{12,0},{1,13},{5,9},{9,5},{13,1},{2,14},{6,10},... | collective-permute-start | bytes 6291464 | tf_op jit(solution)/shard_map/ppermute | solution.py:127
  250.7 100.9 %collective-permute-start.9 = (bf16[1024,1024]{1,0:T(8,128)(2,1)}, bf16[1024,1024]{1,0:T(8,128)(2,1)}, u32[]{:S(2)}, u32[]{:S(2)}) collective-permute-start(bf16[1024,1024]{1,0:T(8,128)(2,1)} %get-tuple-element.36), channel_id=1, source_target_pairs={{0,4},{4,0},{8,12},{12,8},{1,5},{5,1},{9,13},{13,9},{2,6},{6,2},{1... | collective-permute-start | bytes 6291464 | tf_op jit(solution)/shard_map/ppermute | solution.py:127
  260.2 93.1 %collective-permute-start.6 = (bf16[1024,1024]{1,0:T(8,128)(2,1)}, bf16[1024,1024]{1,0:T(8,128)(2,1)}, u32[]{:S(2)}, u32[]{:S(2)}) collective-permute-start(bf16[1024,1024]{1,0:T(8,128)(2,1)} %get-tuple-element.32), channel_id=1, source_target_pairs={{0,4},{4,0},{8,12},{12,8},{1,5},{5,1},{9,13},{13,9},{2,6},{6,2},{1... | collective-permute-start | bytes 6291464 | tf_op jit(solution)/shard_map/ppermute | solution.py:127
  260.2 127.5 %collective-permute-start.7 = (bf16[1024,1024]{1,0:T(8,128)(2,1)}, bf16[1024,1024]{1,0:T(8,128)(2,1)}, u32[]{:S(2)}, u32[]{:S(2)}) collective-permute-start(bf16[1024,1024]{1,0:T(8,128)(2,1)} %get-tuple-element.33), channel_id=1, source_target_pairs={{0,8},{4,12},{8,0},{12,4},{1,9},{5,13},{9,1},{13,5},{2,10},{6,14},... | collective-permute-start | bytes 6291464 | tf_op jit(solution)/shard_map/ppermute | solution.py:127
  297.8 134.1 %collective-permute-start.8 = (bf16[1024,1024]{1,0:T(8,128)(2,1)}, bf16[1024,1024]{1,0:T(8,128)(2,1)}, u32[]{:S(2)}, u32[]{:S(2)}) collective-permute-start(bf16[1024,1024]{1,0:T(8,128)(2,1)} %get-tuple-element.34), channel_id=1, source_target_pairs={{0,12},{4,8},{8,4},{12,0},{1,13},{5,9},{9,5},{13,1},{2,14},{6,10},... | collective-permute-start | bytes 6291464 | tf_op jit(solution)/shard_map/ppermute | solution.py:127
  342.0 91.1 %collective-permute-start.3 = (bf16[1024,1024]{1,0:T(8,128)(2,1)}, bf16[1024,1024]{1,0:T(8,128)(2,1)}, u32[]{:S(2)}, u32[]{:S(2)}) collective-permute-start(bf16[1024,1024]{1,0:T(8,128)(2,1)} %get-tuple-element.28), channel_id=1, source_target_pairs={{0,4},{4,0},{8,12},{12,8},{1,5},{5,1},{9,13},{13,9},{2,6},{6,2},{1... | collective-permute-start | bytes 6291464 | tf_op jit(solution)/shard_map/ppermute | solution.py:127
  351.6 125.9 %collective-permute-start.4 = (bf16[1024,1024]{1,0:T(8,128)(2,1)}, bf16[1024,1024]{1,0:T(8,128)(2,1)S(1)}, u32[]{:S(2)}, u32[]{:S(2)}) collective-permute-start(bf16[1024,1024]{1,0:T(8,128)(2,1)} %get-tuple-element.29), channel_id=1, source_target_pairs={{0,8},{4,12},{8,0},{12,4},{1,9},{5,13},{9,1},{13,5},{2,10},{6,14},... | collective-permute-start | bytes 6291464 | tf_op jit(solution)/shard_map/ppermute | solution.py:127
  353.3 168.5 %collective-permute-start.5 = (bf16[1024,1024]{1,0:T(8,128)(2,1)}, bf16[1024,1024]{1,0:T(8,128)(2,1)}, u32[]{:S(2)}, u32[]{:S(2)}) collective-permute-start(bf16[1024,1024]{1,0:T(8,128)(2,1)} %get-tuple-element.30), channel_id=1, source_target_pairs={{0,12},{4,8},{8,4},{12,0},{1,13},{5,9},{9,5},{13,1},{2,14},{6,10},... | collective-permute-start | bytes 6291464 | tf_op jit(solution)/shard_map/ppermute | solution.py:127
  387.8 135.2 %collective-permute-start = (bf16[1024,1024]{1,0:T(8,128)(2,1)}, bf16[1024,1024]{1,0:T(8,128)(2,1)}, u32[]{:S(2)}, u32[]{:S(2)}) collective-permute-start(bf16[1024,1024]{1,0:T(8,128)(2,1)} %get-tuple-element.24), channel_id=1, source_target_pairs={{0,4},{4,0},{8,12},{12,8},{1,5},{5,1},{9,13},{13,9},{2,6},{6,2},{1... | collective-permute-start | bytes 6291464 | tf_op jit(solution)/shard_map/ppermute | solution.py:127
  431.9 135.7 %collective-permute-start.1 = (bf16[1024,1024]{1,0:T(8,128)(2,1)}, bf16[1024,1024]{1,0:T(8,128)(2,1)}, u32[]{:S(2)}, u32[]{:S(2)}) collective-permute-start(bf16[1024,1024]{1,0:T(8,128)(2,1)} %get-tuple-element.25), channel_id=1, source_target_pairs={{0,8},{4,12},{8,0},{12,4},{1,9},{5,13},{9,1},{13,5},{2,10},{6,14},... | collective-permute-start | bytes 6291464 | tf_op jit(solution)/shard_map/ppermute | solution.py:127
  433.1 178.5 %collective-permute-start.2 = (bf16[1024,1024]{1,0:T(8,128)(2,1)}, bf16[1024,1024]{1,0:T(8,128)(2,1)}, u32[]{:S(2)}, u32[]{:S(2)}) collective-permute-start(bf16[1024,1024]{1,0:T(8,128)(2,1)} %get-tuple-element.26), channel_id=1, source_target_pairs={{0,12},{4,8},{8,4},{12,0},{1,13},{5,9},{9,5},{13,1},{2,14},{6,10},... | collective-permute-start | bytes 6291464 | tf_op jit(solution)/shard_map/ppermute | solution.py:127
  477.5 142.5 %collective-permute-start.18 = (bf16[256,1024]{1,0:T(8,128)(2,1)}, bf16[256,1024]{1,0:T(8,128)(2,1)S(1)}, u32[]{:S(2)}, u32[]{:S(2)}) collective-permute-start(bf16[256,1024]{1,0:T(8,128)(2,1)} %get-tuple-element.40), channel_id=1, source_target_pairs={{0,4},{4,0},{8,12},{12,8},{1,5},{5,1},{9,13},{13,9},{2,6},{6,2},{1... | collective-permute-start | bytes 1572872 | tf_op jit(solution)/shard_map/ppermute | solution.py:127
  521.8 101.8 %collective-permute-start.19 = (bf16[256,1024]{1,0:T(8,128)(2,1)}, bf16[256,1024]{1,0:T(8,128)(2,1)S(1)}, u32[]{:S(2)}, u32[]{:S(2)}) collective-permute-start(bf16[256,1024]{1,0:T(8,128)(2,1)} %get-tuple-element.41), channel_id=1, source_target_pairs={{0,8},{4,12},{8,0},{12,4},{1,9},{5,13},{9,1},{13,5},{2,10},{6,14},... | collective-permute-start | bytes 1572872 | tf_op jit(solution)/shard_map/ppermute | solution.py:127
  523.0 110.5 %collective-permute-start.20 = (bf16[256,1024]{1,0:T(8,128)(2,1)}, bf16[256,1024]{1,0:T(8,128)(2,1)}, u32[]{:S(2)}, u32[]{:S(2)}) collective-permute-start(bf16[256,1024]{1,0:T(8,128)(2,1)} %get-tuple-element.42), channel_id=1, source_target_pairs={{0,12},{4,8},{8,4},{12,0},{1,13},{5,9},{9,5},{13,1},{2,14},{6,10},... | collective-permute-start | bytes 1572872 | tf_op jit(solution)/shard_map/ppermute | solution.py:127
  (8 other events, 138.6 us)
Sparse Core Ops, SparseCore 0:
  106.5 281.9 reduce-scatter.2
  390.8 77.3 reduce-scatter.4
